TPU v7x, 32 devices: a 4x4x1 block of a 4x4x8 slice. The times are simulated.
32 devices in a mesh: data: 1 (over z), model: 4 (over y), time: 8 (over x, core).
Axes of the slice: x: 4, y: 4, z: 1, core: 2. Of those that a mesh axis runs over, the one named last changes fastest.
The devices are a block of a 4x4x8 slice.
Arguments:
- x_init: float32 [64, 16, 256], P('data')
- w_up: bfloat16 [256, 1152], P(None, 'model')
- w_down: bfloat16 [1152, 256], P('model')
- mod_scale: bfloat16 [128, 1152], P('time', 'model')
- mod_shift: bfloat16 [128, 1152], P('time', 'model')
- step_size: float32 [128], P('time')
Outputs:
- output: float32 [128, 64, 16, 256], P('time', 'data')
All inputs are finite; a program needn't handle non-finite values.
Results may differ from a plain program's by a relative error of at most 0.001.
Values are sent between devices in bfloat16 or wider.
A program may use at most 768 MiB of HBM per device.

v0:
```python
import jax
import jax.numpy as jnp
from jax import lax
from jax.sharding import PartitionSpec as P

SWEEPS = 4


def local_drift(latents, w_up, w_down, scale_f, shift_f):
    pre_act = jnp.einsum('tbnc,cd->tbnd', latents.astype(jnp.bfloat16), w_up, preferred_element_type=jnp.float32)
    hidden = jax.nn.gelu(pre_act * scale_f[:, None, None, :] + shift_f[:, None, None, :], approximate=True)
    return jnp.einsum('tbnd,dc->tbnc', hidden.astype(jnp.bfloat16), w_down, preferred_element_type=jnp.float32)


def solution(mesh):
    time_devs = mesh.shape['time']

    def device_body(x_init, w_up, w_down, mod_scale, mod_shift, step_size):
        scale_f = 1.0 + mod_scale.astype(jnp.float32)
        shift_f = mod_shift.astype(jnp.float32)
        step_col = step_size[:, None, None, None]
        latents = jnp.broadcast_to(x_init[None], (mod_scale.shape[0],) + x_init.shape)
        for sweep_idx in range(SWEEPS):
            part_drift = local_drift(latents, w_up, w_down, scale_f, shift_f)
            drifts = step_col * lax.psum(part_drift, 'model')
            running = jnp.cumsum(drifts, axis=0)
            dev_total = running[-1]
            scan_acc = dev_total
            shift_len = 1
            while shift_len < time_devs:
                perm_pairs = [(source_idx, source_idx + shift_len) for source_idx in range(time_devs - shift_len)]
                scan_acc = scan_acc + lax.ppermute(scan_acc, 'time', perm_pairs)
                shift_len = shift_len * 2
            offset = scan_acc - dev_total
            latents = (x_init + offset)[None] + (running - drifts)
        return latents

    return jax.shard_map(device_body, mesh=mesh, in_specs=(P('data', None, None), P(None, 'model'), P('model', None), P('time', 'model'), P('time', 'model'), P('time')), out_specs=P('time', 'data', None, None), check_vma=False)
```

profile of v0, /device:TPU:96, one launch (start us, length us, event | category | flops | bytes accessed | tf_op | source)
XLA Modules:
  0.0 1627.7 jit_solution(17240450900038518795)
XLA Ops:
  9.3 16.6 %fusion.46 = f32[16,64,16,256]{3,2,1,0:T(8,128)} fusion(f32[16,288]{1,0:T(8,128)S(1)} %convert_element_type.33, f32[16,288]{1,0:T(8,128)S(1)} %convert_add_fusion, bf16[64,16,256]{2,1,0:T(8,128)(2,1)S(1)} %convert_element_type.31, bf16[288,256]{1,0:T(8,128)(2,1)S(1)} %copy-done, bf16[256,288]{0,1:T(8,128)(2,1)} %param.7), kind=kOutput, calls=%fused_computation.51 | convolution fusion | flops 4883742720 | bytes 17633280 | tf_op jit(solution)/shard_map/tbnd,dc->tbnc/dot_general | solution.py:12
  26.1 292.8 %all-reduce.5.cloned.1.call-done = f32[16,64,16,256]{3,2,1,0:T(8,128)} async-done(((f32[16,64,16,256]{3,2,1,0:T(8,128)}), f32[16,64,16,256]{3,2,1,0:T(8,128)}) %all-reduce.5.cloned.1.call-update) | async-done | bytes 16777232 | tf_op jit(solution)/shard_map/psum | solution.py:25
  318.9 13.4 fusion.38
  338.7 15.8 collective-permute-start.1
  354.6 21.6 %collective-permute-done.1 = f32[64,16,256]{2,1,0:T(8,128)S(1)} collective-permute-done((f32[64,16,256]{2,1,0:T(8,128)S(1)}, f32[64,16,256]{2,1,0:T(8,128)S(1)}, u32[]{:S(2)}, u32[]{:S(2)}) %collective-permute-start.1) | collective-permute-done | bytes 1048608 | tf_op jit(solution)/shard_map/ppermute | solution.py:32
  382.3 20.5 %collective-permute-done.2 = f32[64,16,256]{2,1,0:T(8,128)S(1)} collective-permute-done((f32[64,16,256]{2,1,0:T(8,128)S(1)}, f32[64,16,256]{2,1,0:T(8,128)S(1)}, u32[]{:S(2)}, u32[]{:S(2)}) %collective-permute-start.2) | collective-permute-done | bytes 1048608 | tf_op jit(solution)/shard_map/ppermute | solution.py:32
  404.5 23.0 %fusion.44 = f32[16,64,16,256]{3,2,1,0:T(8,128)} fusion(f32[16,288]{1,0:T(8,128)S(1)} %convert_element_type.33, f32[16,288]{1,0:T(8,128)S(1)} %convert_add_fusion, f32[16,64,16,256]{3,2,1,0:T(8,128)} %fusion.38, f32[16,64,16,256]{3,2,1,0:T(8,128)} %all-reduce.5.cloned.1.call-done, f32[64,16,256]{2,1,0:T(8,128)S(1)} %subtract_add_fusion.4, ...), kind=kOutput, calls=%fused_computation.50 | convolution fusion | flops 4900519936 | bytes 51712064 | tf_op jit(solution)/shard_map/tbnd,dc->tbnc/dot_general | solution.py:12
  427.6 291.1 %all-reduce.7.cloned.1.call-done = f32[16,64,16,256]{3,2,1,0:T(8,128)} async-done(((f32[16,64,16,256]{3,2,1,0:T(8,128)}), f32[16,64,16,256]{3,2,1,0:T(8,128)}) %all-reduce.7.cloned.1.call-update) | async-done | bytes 16777232 | tf_op jit(solution)/shard_map/psum | solution.py:25
  718.7 13.4 fusion.36
  738.6 15.8 collective-permute-start.4
  754.4 21.6 %collective-permute-done.4 = f32[64,16,256]{2,1,0:T(8,128)S(1)} collective-permute-done((f32[64,16,256]{2,1,0:T(8,128)S(1)}, f32[64,16,256]{2,1,0:T(8,128)S(1)}, u32[]{:S(2)}, u32[]{:S(2)}) %collective-permute-start.4) | collective-permute-done | bytes 1048608 | tf_op jit(solution)/shard_map/ppermute | solution.py:32
  782.2 20.5 %collective-permute-done.5 = f32[64,16,256]{2,1,0:T(8,128)S(1)} collective-permute-done((f32[64,16,256]{2,1,0:T(8,128)S(1)}, f32[64,16,256]{2,1,0:T(8,128)S(1)}, u32[]{:S(2)}, u32[]{:S(2)}) %collective-permute-start.5) | collective-permute-done | bytes 1048608 | tf_op jit(solution)/shard_map/ppermute | solution.py:32
  804.3 23.0 %fusion.42 = f32[16,64,16,256]{3,2,1,0:T(8,128)} fusion(f32[16,288]{1,0:T(8,128)S(1)} %convert_element_type.33, f32[16,288]{1,0:T(8,128)S(1)} %convert_add_fusion, f32[16,64,16,256]{3,2,1,0:T(8,128)} %fusion.36, f32[16,64,16,256]{3,2,1,0:T(8,128)} %all-reduce.7.cloned.1.call-done, f32[64,16,256]{2,1,0:T(8,128)S(1)} %subtract_add_fusion.3, ...), kind=kOutput, calls=%fused_computation.49 | convolution fusion | flops 4900519936 | bytes 51712064 | tf_op jit(solution)/shard_map/tbnd,dc->tbnc/dot_general | solution.py:12
  827.5 291.1 %all-reduce.9.cloned.1.call-done = f32[16,64,16,256]{3,2,1,0:T(8,128)} async-done(((f32[16,64,16,256]{3,2,1,0:T(8,128)}), f32[16,64,16,256]{3,2,1,0:T(8,128)}) %all-reduce.9.cloned.1.call-update) | async-done | bytes 16777232 | tf_op jit(solution)/shard_map/psum | solution.py:25
  1118.6 13.4 fusion.34
  1138.5 15.8 collective-permute-start.7
  1154.3 21.6 %collective-permute-done.7 = f32[64,16,256]{2,1,0:T(8,128)S(1)} collective-permute-done((f32[64,16,256]{2,1,0:T(8,128)S(1)}, f32[64,16,256]{2,1,0:T(8,128)S(1)}, u32[]{:S(2)}, u32[]{:S(2)}) %collective-permute-start.7) | collective-permute-done | bytes 1048608 | tf_op jit(solution)/shard_map/ppermute | solution.py:32
  1182.1 20.4 %collective-permute-done.8 = f32[64,16,256]{2,1,0:T(8,128)S(1)} collective-permute-done((f32[64,16,256]{2,1,0:T(8,128)S(1)}, f32[64,16,256]{2,1,0:T(8,128)S(1)}, u32[]{:S(2)}, u32[]{:S(2)}) %collective-permute-start.8) | collective-permute-done | bytes 1048608 | tf_op jit(solution)/shard_map/ppermute | solution.py:32
  1204.2 23.0 %fusion.40 = f32[16,64,16,256]{3,2,1,0:T(8,128)} fusion(f32[16,288]{1,0:T(8,128)S(1)} %convert_element_type.33, f32[16,288]{1,0:T(8,128)S(1)} %convert_add_fusion, f32[16,64,16,256]{3,2,1,0:T(8,128)} %fusion.34, f32[16,64,16,256]{3,2,1,0:T(8,128)} %all-reduce.9.cloned.1.call-done, f32[64,16,256]{2,1,0:T(8,128)S(1)} %subtract_add_fusion.2, ...), kind=kOutput, calls=%fused_computation.48 | convolution fusion | flops 4900519936 | bytes 51712064 | tf_op jit(solution)/shard_map/tbnd,dc->tbnc/dot_general | solution.py:12
  1227.3 291.2 %all-reduce.11.cloned.1.call-done = f32[16,64,16,256]{3,2,1,0:T(8,128)} async-done(((f32[16,64,16,256]{3,2,1,0:T(8,128)}), f32[16,64,16,256]{3,2,1,0:T(8,128)}) %all-reduce.11.cloned.1.call-update) | async-done | bytes 16777232 | tf_op jit(solution)/shard_map/psum | solution.py:25
  1538.4 15.8 collective-permute-start.10
  1554.2 21.6 %collective-permute-done.10 = f32[64,16,256]{2,1,0:T(8,128)S(1)} collective-permute-done((f32[64,16,256]{2,1,0:T(8,128)S(1)}, f32[64,16,256]{2,1,0:T(8,128)S(1)}, u32[]{:S(2)}, u32[]{:S(2)}) %collective-permute-start.10) | collective-permute-done | bytes 1048608 | tf_op jit(solution)/shard_map/ppermute | solution.py:32
  1581.7 20.7 %collective-permute-done.11 = f32[64,16,256]{2,1,0:T(8,128)S(1)} collective-permute-done((f32[64,16,256]{2,1,0:T(8,128)S(1)}, f32[64,16,256]{2,1,0:T(8,128)S(1)}, u32[]{:S(2)}, u32[]{:S(2)}) %collective-permute-start.11) | collective-permute-done | bytes 1048608 | tf_op jit(solution)/shard_map/ppermute | solution.py:32
  1604.1 17.1 %subtract_add_fusion = f32[16,64,16,256]{3,2,1,0:T(8,128)} fusion(f32[16,64,16,256]{3,2,1,0:T(8,128)} %fusion.32, f32[16,64,16,256]{3,2,1,0:T(8,128)} %all-reduce.11.cloned.1.call-done, f32[64,16,256]{2,1,0:T(8,128)S(1)} %subtract_add_fusion.1, f32[16]{0:T(128)S(1)} %copy-done.2), kind=kLoop, calls=%fused_computation.36 | loop fusion | flops 12582912 | bytes 51380288 | tf_op jit(solution)/shard_map/add | solution.py:35
  (48 shorter events, 73.9 us)
Async XLA Ops:
  6.5 2.8 copy-start
  6.6 312.3 %all-reduce.5.cloned.1.call-start = ((), (), s32[]{:S(2)}) async-start(), calls=%async_computation | async-start | bytes 33554432 | tf_op jit(solution)/shard_map/psum | solution.py:25
  25.9 293.0 %copy-start.2 = (f32[16]{0:T(128)S(1)}, f32[16]{0:T(128)}, u32[]{:S(2)}) copy-start(f32[16]{0:T(128)} %param.11) | copy-start | bytes 196
  26.0 376.8 %copy-start.1 = (f32[64,16,256]{2,1,0:T(8,128)S(1)}, f32[64,16,256]{2,1,0:T(8,128)}, u32[]{:S(2)}) copy-start(f32[64,16,256]{2,1,0:T(8,128)} %param.6) | copy-start | bytes 3145732
  26.0 378.5 %copy-start.3 = (bf16[256,288]{0,1:T(8,128)(2,1)S(1)}, bf16[256,288]{0,1:T(8,128)(2,1)}, u32[]{:S(2)}) copy-start(bf16[256,288]{0,1:T(8,128)(2,1)} %param.7) | copy-start | bytes 442372
  26.0 692.7 %all-reduce.7.cloned.1.call-start = ((), (), s32[]{:S(2)}) async-start(), calls=%async_computation.1 | async-start | bytes 33554432 | tf_op jit(solution)/shard_map/psum | solution.py:25
  333.5 3.8 collective-permute-start
  338.7 37.4 %collective-permute-start.1 = (f32[64,16,256]{2,1,0:T(8,128)S(1)}, f32[64,16,256]{2,1,0:T(8,128)S(1)}, u32[]{:S(2)}, u32[]{:S(2)}) collective-permute-start(f32[64,16,256]{2,1,0:T(8,128)S(1)} %fusion.99), channel_id=1, source_target_pairs={{0,2},{1,3},{2,4},{3,5},{4,6},{5,7},{8,10},{9,11},{10,12},{11,13},... | collective-permute-start | bytes 3145736 | tf_op jit(solution)/shard_map/ppermute | solution.py:32
  376.3 26.4 %collective-permute-start.2 = (f32[64,16,256]{2,1,0:T(8,128)S(1)}, f32[64,16,256]{2,1,0:T(8,128)S(1)}, u32[]{:S(2)}, u32[]{:S(2)}) collective-permute-start(f32[64,16,256]{2,1,0:T(8,128)S(1)} %add.151), channel_id=1, source_target_pairs={{0,4},{1,5},{2,6},{3,7},{8,12},{9,13},{10,14},{11,15},{16,20},{17,... | collective-permute-start | bytes 3145736 | tf_op jit(solution)/shard_map/ppermute | solution.py:32
  427.5 691.1 %all-reduce.9.cloned.1.call-start = ((), (), s32[]{:S(2)}) async-start(), calls=%async_computation.2 | async-start | bytes 33554432 | tf_op jit(solution)/shard_map/psum | solution.py:25
  733.4 3.8 collective-permute-start.3
  738.6 37.4 %collective-permute-start.4 = (f32[64,16,256]{2,1,0:T(8,128)S(1)}, f32[64,16,256]{2,1,0:T(8,128)S(1)}, u32[]{:S(2)}, u32[]{:S(2)}) collective-permute-start(f32[64,16,256]{2,1,0:T(8,128)S(1)} %fusion.100), channel_id=1, source_target_pairs={{0,2},{1,3},{2,4},{3,5},{4,6},{5,7},{8,10},{9,11},{10,12},{11,13},... | collective-permute-start | bytes 3145736 | tf_op jit(solution)/shard_map/ppermute | solution.py:32
  776.2 26.4 %collective-permute-start.5 = (f32[64,16,256]{2,1,0:T(8,128)S(1)}, f32[64,16,256]{2,1,0:T(8,128)S(1)}, u32[]{:S(2)}, u32[]{:S(2)}) collective-permute-start(f32[64,16,256]{2,1,0:T(8,128)S(1)} %add.160), channel_id=1, source_target_pairs={{0,4},{1,5},{2,6},{3,7},{8,12},{9,13},{10,14},{11,15},{16,20},{17,... | collective-permute-start | bytes 3145736 | tf_op jit(solution)/shard_map/ppermute | solution.py:32
  827.4 691.1 %all-reduce.11.cloned.1.call-start = ((), (), s32[]{:S(2)}) async-start(), calls=%async_computation.3 | async-start | bytes 33554432 | tf_op jit(solution)/shard_map/psum | solution.py:25
  1133.3 3.8 collective-permute-start.6
  1138.5 37.4 %collective-permute-start.7 = (f32[64,16,256]{2,1,0:T(8,128)S(1)}, f32[64,16,256]{2,1,0:T(8,128)S(1)}, u32[]{:S(2)}, u32[]{:S(2)}) collective-permute-start(f32[64,16,256]{2,1,0:T(8,128)S(1)} %fusion.101), channel_id=1, source_target_pairs={{0,2},{1,3},{2,4},{3,5},{4,6},{5,7},{8,10},{9,11},{10,12},{11,13},... | collective-permute-start | bytes 3145736 | tf_op jit(solution)/shard_map/ppermute | solution.py:32
  1176.1 26.4 %collective-permute-start.8 = (f32[64,16,256]{2,1,0:T(8,128)S(1)}, f32[64,16,256]{2,1,0:T(8,128)S(1)}, u32[]{:S(2)}, u32[]{:S(2)}) collective-permute-start(f32[64,16,256]{2,1,0:T(8,128)S(1)} %add.169), channel_id=1, source_target_pairs={{0,4},{1,5},{2,6},{3,7},{8,12},{9,13},{10,14},{11,15},{16,20},{17,... | collective-permute-start | bytes 3145736 | tf_op jit(solution)/shard_map/ppermute | solution.py:32
  1533.1 3.8 collective-permute-start.9
  1538.4 37.4 %collective-permute-start.10 = (f32[64,16,256]{2,1,0:T(8,128)S(1)}, f32[64,16,256]{2,1,0:T(8,128)S(1)}, u32[]{:S(2)}, u32[]{:S(2)}) collective-permute-start(f32[64,16,256]{2,1,0:T(8,128)S(1)} %fusion.102), channel_id=1, source_target_pairs={{0,2},{1,3},{2,4},{3,5},{4,6},{5,7},{8,10},{9,11},{10,12},{11,13},... | collective-permute-start | bytes 3145736 | tf_op jit(solution)/shard_map/ppermute | solution.py:32
  1576.0 26.4 %collective-permute-start.11 = (f32[64,16,256]{2,1,0:T(8,128)S(1)}, f32[64,16,256]{2,1,0:T(8,128)S(1)}, u32[]{:S(2)}, u32[]{:S(2)}) collective-permute-start(f32[64,16,256]{2,1,0:T(8,128)S(1)} %add.178), channel_id=1, source_target_pairs={{0,4},{1,5},{2,6},{3,7},{8,12},{9,13},{10,14},{11,15},{16,20},{17,... | collective-permute-start | bytes 3145736 | tf_op jit(solution)/shard_map/ppermute | solution.py:32
Sparse Core Ops, SparseCore 0:
  26.1 292.7 all-reduce.4
  427.6 291.0 all-reduce.6
  827.5 291.0 all-reduce.8
  1227.4 291.0 all-reduce.10
where the time goes:
time: 1630 us
  waiting for transfers between devices  1340 us (82%)
  starting transfers between devices  93.4 us (6%)
  other arithmetic  86.7 us (5%)
  matrix products  85.5 us (5%)
    psum x4, waiting for transfers between devices, device_body(): drifts = step_col * lax.psum(part_drift, 'model')  1170 us
    ppermute x12, waiting for transfers between devices, device_body(): scan_acc = scan_acc + lax.ppermute(scan_acc, 'time', perm_pairs)  177 us
    ppermute x12, starting transfers between devices, device_body(): scan_acc = scan_acc + lax.ppermute(scan_acc, 'time', perm_pairs)  93.2 us
    dot_general x4, matrix products, local_drift(): jnp.einsum('tbnd,dc->tbnc', hidden.astype(jnp.bfloat16), w_down, preferre...  85.5 us
    another operation x4, other arithmetic, device_body(): running = jnp.cumsum(drifts, axis=0)  53.4 us
  transfers between devices with their start and end apart: 16, of which 16 were waited for; matrix products, arithmetic and copies ran while one was open for 0% of the time, Pallas kernels for 0%

commit v1 on v0

v1 whole, which is shorter than its diff:
```python
import functools
import math

import jax
import jax.numpy as jnp
from jax import lax
from jax.experimental import pallas as pl
from jax.experimental.pallas import tpu as pltpu
from jax.sharding import PartitionSpec as P

SWEEPS = 4
ROWS = 16
STAGES = 4
F32, BF16 = jnp.float32, jnp.bfloat16
MESH_ID = pl.DeviceIdType.MESH
ROOT = math.sqrt(2.0 / math.pi)


def kernel(n_t, n_m, h_ref, x0_ref, w1_ref, w2_ref, sc_ref, sh_ref, out_ref, xbuf, obuf, rbuf, robuf, gbuf, stage,
           s1s, s1r, s2s, s2r, s3s, s3r, o1s, o1r, o2s, o2r, o3s, o3r, out_sem):
    me_t = lax.axis_index('time')
    me_m = lax.axis_index('model')
    n_k = xbuf.shape[0]
    span = xbuf.shape[2] // ROWS
    half = xbuf.shape[2] // 2
    hid = w1_ref.shape[1]
    n_x = n_t // 2
    up, down = lax.rem(me_m + 1, n_m), lax.rem(me_m + n_m - 1, n_m)
    chunks = [(lo, min(lo + 256, hid)) for lo in range(0, hid, 256)]

    def peer(q, sign):
        qx, dc = q // 2, q % 2
        dx = qx + (qx // 2) * (5 - 2 * qx)
        return ((me_t // 2 + n_x + sign * dx) % n_x) * 2 + (me_t % 2 + dc) % 2

    def remote(src, dst, send, recv, **where):
        return pltpu.make_async_remote_copy(src_ref=src, dst_ref=dst, send_sem=send, recv_sem=recv, device_id=where, device_id_type=MESH_ID)

    def drift(x, tb, same):
        for lo, hi in chunks:
            p = jnp.dot(x, w1_ref[:, lo:hi], preferred_element_type=F32)
            for j in range(span):
                pj = p if same else p[j * ROWS:(j + 1) * ROWS]
                v = pj * sc_ref[tb, j:j + 1, lo:hi] + sh_ref[tb, j:j + 1, lo:hi]
                t = jnp.tanh(v * (2 * ROOT + (8 * 0.044715 * ROOT) * (v * v)))
                gbuf[j * ROWS:(j + 1) * ROWS, lo:hi] = (v + v * t).astype(BF16)
        return jnp.dot(gbuf[...], w2_ref[...], preferred_element_type=F32)

    def sweep(k, number):
        x0 = x0_ref[pl.ds(((me_m * n_t + me_t) * n_k + k) * ROWS, ROWS), :]

        def body(tb, acc):
            if number == 0:
                f = drift(x0.astype(BF16), tb, True)
            else:
                f = drift(xbuf[k, tb], tb, False)
            if number == SWEEPS - 1:
                obuf[k, tb] = acc
            for j in range(span):
                if number < SWEEPS - 1:
                    xbuf[k, tb, j * ROWS:(j + 1) * ROWS, :] = (x0 + acc).astype(BF16)
                acc = acc + h_ref[tb * span + j] * f[j * ROWS:(j + 1) * ROWS]
            return acc

        lax.fori_loop(0, n_t, body, jnp.zeros_like(x0))

    def x_send(k):
        @pl.loop(1, n_t)
        def _(q):
            to = peer(q, 1)
            remote(xbuf.at[k, to], rbuf.at[0, k, me_t], s1s.at[k, q], s1r.at[k, q], time=to).start()
        rbuf[0, k, me_t] = xbuf[k, me_t]

    def x_row(q, k):
        src = peer(q, -1)

        @pl.when(q > 0)
        def _():
            remote(xbuf.at[k, 0], rbuf.at[0, k, src], s1s.at[k, q], s1r.at[k, q], time=src).wait_recv()
        i = k * n_t + q
        remote(rbuf.at[0, k, src], rbuf.at[1, k, src], s2s.at[0, i], s2r.at[0, i], model=up).start()
        remote(rbuf.at[0, k, src], rbuf.at[2, k, src], s2s.at[1, i], s2r.at[1, i], model=down).start()

    def x_pass(q, k):
        src = peer(q, -1)
        i = k * n_t + q
        for d, to in ((0, up), (1, down)):
            remote(rbuf.at[0, k, src], rbuf.at[1 + d, k, src], s2s.at[d, i], s2r.at[d, i], model=to).wait_recv()
            part = pl.ds(d * half, half)
            remote(rbuf.at[1 + d, k, src, part], rbuf.at[3, k, src, part], s3s.at[d, i], s3r.at[d, i], model=to).start()

    def x_far(q, k):
        src = peer(q, -1)
        i = k * n_t + q
        for d, to in ((0, up), (1, down)):
            part = pl.ds(d * half, half)
            remote(rbuf.at[1 + d, k, src, part], rbuf.at[3, k, src, part], s3s.at[d, i], s3r.at[d, i], model=to).wait_recv()

    def o_send(k):
        @pl.loop(1, n_t)
        def _(q):
            to = peer(q, 1)
            remote(obuf.at[k, to], robuf.at[0, k, me_t], o1s.at[k, q], o1r.at[k, q], time=to).start()
        robuf[0, k, me_t] = obuf[k, me_t]

    def o_row(k):
        @pl.loop(1, n_t)
        def _(q):
            src = peer(q, -1)
            remote(obuf.at[k, 0], robuf.at[0, k, src], o1s.at[k, q], o1r.at[k, q], time=src).wait_recv()
        remote(robuf.at[0, k], robuf.at[1, k], o2s.at[0, k], o2r.at[0, k], model=up).start()
        remote(robuf.at[0, k], robuf.at[2, k], o2s.at[1, k], o2r.at[1, k], model=down).start()

    def o_pass(k):
        for d, to in ((0, up), (1, down)):
            remote(robuf.at[0, k], robuf.at[1 + d, k], o2s.at[d, k], o2r.at[d, k], model=to).wait_recv()
            part = pl.ds(d * n_x, n_x)
            remote(robuf.at[1 + d, k, part], robuf.at[3, k, part], o3s.at[d, k], o3r.at[d, k], model=to).start()

    def o_far(k):
        for d, to in ((0, up), (1, down)):
            part = pl.ds(d * n_x, n_x)
            remote(robuf.at[1 + d, k, part], robuf.at[3, k, part], o3s.at[d, k], o3r.at[d, k], model=to).wait_recv()

    def out_copy(slot, row):
        return pltpu.make_async_copy(stage.at[slot], out_ref.at[:, pl.ds(row, ROWS), :], out_sem.at[slot])

    def finish(rel, q, k, number):
        src = peer(q, -1)
        origin = (me_m + (n_m - rel) + (rel // 2) * (2 * rel - 5)) % n_m
        row = ((origin * n_t + src) * n_k + k) * ROWS
        slot = number % STAGES

        @pl.when(number >= STAGES)
        def _():
            out_copy(slot, 0).wait()
        f = drift(rbuf[rel, k, src], me_t, False)
        x0 = x0_ref[pl.ds(row, ROWS), :]
        acc = robuf[rel, k, src]
        for j in range(span):
            stage[slot, j] = x0 + acc
            acc = acc + h_ref[me_t * span + j] * f[j * ROWS:(j + 1) * ROWS]
        out_copy(slot, row).start()

    barrier = pltpu.get_barrier_semaphore()

    @pl.loop(1, n_t)
    def _(q):
        pl.semaphore_signal(barrier, inc=1, device_id={'time': peer(q, 1)}, device_id_type=MESH_ID)
    for to in (up, down):
        pl.semaphore_signal(barrier, inc=1, device_id={'model': to}, device_id_type=MESH_ID)
    pl.semaphore_wait(barrier, n_t + 1)

    for number in range(SWEEPS - 1):
        sweep(0, number)
    x_send(0)
    x_row(0, 0)
    sweep(0, SWEEPS - 1)
    o_send(0)
    x_row(1, 0)
    sweep(1, 0)
    x_row(2, 0)
    x_row(3, 0)
    x_pass(0, 0)
    sweep(1, 1)
    x_row(4, 0)
    x_row(5, 0)
    x_pass(1, 0)
    o_row(0)
    sweep(1, 2)
    x_send(1)
    x_row(6, 0)
    x_row(7, 0)
    x_pass(2, 0)
    o_pass(0)
    sweep(1, SWEEPS - 1)
    o_send(1)
    x_pass(3, 0)
    o_far(0)

    early = 4

    @pl.loop(0, n_k * n_t)
    def _(i):
        k, q = i // n_t, i % n_t

        @pl.when(i >= early)
        def _():
            x_pass(q, k)

        @pl.when(i < n_t)
        def _():
            x_row(q, 1)

        @pl.when(i == 2)
        def _():
            o_row(1)

        @pl.when(i == 5)
        def _():
            o_pass(1)

        @pl.when(i == n_t)
        def _():
            o_far(1)

        @pl.loop(0, n_m)
        def _(rel):
            @pl.when(rel == n_m - 1)
            def _():
                x_far(q, k)
            finish(rel, q, k, i * n_m + rel)

    for slot in range(STAGES):
        out_copy(slot, 0).wait()

    @pl.loop(0, n_k * n_t)
    def _(i):
        k, q = i // n_t, i % n_t

        @pl.when(q > 0)
        def _():
            remote(xbuf.at[k, 0], rbuf.at[0, k, 0], s1s.at[k, q], s1r.at[k, q], time=peer(q, 1)).wait_send()
            remote(obuf.at[k, 0], robuf.at[0, k, 0], o1s.at[k, q], o1r.at[k, q], time=peer(q, 1)).wait_send()
        for d, to in ((0, up), (1, down)):
            part = pl.ds(d * half, half)
            remote(rbuf.at[0, k, 0], rbuf.at[1 + d, k, 0], s2s.at[d, i], s2r.at[d, i], model=to).wait_send()
            remote(rbuf.at[1 + d, k, 0, part], rbuf.at[3, k, 0, part], s3s.at[d, i], s3r.at[d, i], model=to).wait_send()
    for k in range(n_k):
        for d, to in ((0, up), (1, down)):
            part = pl.ds(d * n_x, n_x)
            remote(robuf.at[0, k], robuf.at[1 + d, k], o2s.at[d, k], o2r.at[d, k], model=to).wait_send()
            remote(robuf.at[1 + d, k, part], robuf.at[3, k, part], o3s.at[d, k], o3r.at[d, k], model=to).wait_send()


def solution(mesh):
    n_t, n_m = mesh.shape['time'], mesh.shape['model']

    def device_body(x_init, w_up, w_down, mod_scale, mod_shift, step_size):
        span, chan = mod_scale.shape[0], x_init.shape[-1]
        rows = x_init.shape[0] * x_init.shape[1]
        w1 = lax.all_gather(w_up, 'model', axis=1, tiled=True)
        w2 = lax.all_gather(w_down, 'model', axis=0, tiled=True)
        mods = jnp.stack([mod_scale, mod_shift])
        mods = lax.all_gather(lax.all_gather(mods, 'model', axis=2, tiled=True), 'time', axis=1, tiled=True).astype(F32)
        mods = mods.reshape(2, n_t, span, -1)
        scale, shift = 0.5 * (1.0 + mods[0]), 0.5 * mods[1]
        steps = lax.all_gather(step_size, 'time', axis=0, tiled=True)
        hid = w1.shape[1]
        n_k = rows // (n_t * n_m * ROWS)
        vmem = pl.BlockSpec(memory_space=pltpu.VMEM)
        sem = lambda *shape: pltpu.SemaphoreType.DMA(shape)
        out = pl.pallas_call(
            functools.partial(kernel, n_t, n_m),
            out_shape=jax.ShapeDtypeStruct((span, rows, chan), F32),
            in_specs=[pl.BlockSpec(memory_space=pltpu.SMEM)] + [vmem] * 5,
            out_specs=pl.BlockSpec(memory_space=pl.ANY),
            scratch_shapes=[
                pltpu.VMEM((n_k, n_t, span * ROWS, chan), BF16),
                pltpu.VMEM((n_k, n_t, ROWS, chan), F32),
                pltpu.VMEM((n_m, n_k, n_t, span * ROWS, chan), BF16),
                pltpu.VMEM((n_m, n_k, n_t, ROWS, chan), F32),
                pltpu.VMEM((span * ROWS, hid), BF16),
                pltpu.VMEM((STAGES, span, ROWS, chan), F32),
                sem(n_k, n_t), sem(n_k, n_t),
                sem(2, n_k * n_t), sem(2, n_k * n_t), sem(2, n_k * n_t), sem(2, n_k * n_t),
                sem(n_k, n_t), sem(n_k, n_t),
                sem(2, n_k), sem(2, n_k), sem(2, n_k), sem(2, n_k),
                sem(STAGES),
            ],
            compiler_params=pltpu.CompilerParams(collective_id=0, has_side_effects=True, vmem_limit_bytes=48 << 20),
        )(steps, x_init.reshape(rows, chan), w1, w2, scale, shift)
        return out.reshape((span,) + x_init.shape)

    return jax.shard_map(device_body, mesh=mesh, in_specs=(P('data', None, None), P(None, 'model'), P('model', None), P('time', 'model'), P('time', 'model'), P('time')), out_specs=P('time', 'data', None, None), check_vma=False)
```

time: 1630 us -> 234 us (0.14)
  waiting for transfers between devices: 1340 us -> 0 us
  Pallas kernels: 0 us -> 137 us
  starting transfers between devices: 93.4 us -> 0 us
  matrix products: 85.5 us -> 0 us
  other arithmetic: 86.7 us -> 2.25 us
  blocking collectives: 0 us -> 77.2 us
    psum x4 -> x0, waiting for transfers between devices: 1170 us -> none  [device_body(): drifts = step_col * lax.psum(part_drift, 'model')]
    ppermute x12 -> x0, waiting for transfers between devices: 177 us -> none  [device_body(): scan_acc = scan_acc + lax.ppermute(scan_acc, 'time', perm_pairs)]
    pallas_call x0 -> x1, Pallas kernels: none -> 137 us  [device_body(): pl.pallas_call(functools.partial(kernel, n_t, n_m), out_shape=jax.ShapeDt...]
    ppermute x12 -> x0, starting transfers between devices: 93.2 us -> none  [device_body(): scan_acc = scan_acc + lax.ppermute(scan_acc, 'time', perm_pairs)]
    dot_general x4 -> x0, matrix products: 85.5 us -> none  [local_drift(): jnp.einsum('tbnd,dc->tbnc', hidden.astype(jnp.bfloat16), w_down, preferre...]
    all_gather x0 -> x4, blocking collectives: none -> 62.8 us  [the longest x1 21.4 us: device_body(): lax.all_gather(lax.all_gather(mods, 'model', axis=2, tiled=True), 'time',...]
    another operation x4 -> x1, other arithmetic: 53.4 us -> 0.73 us  [device_body(): mods = jnp.stack([mod_scale, mod_shift])]
    add x14 -> x0, other arithmetic: 31.2 us -> none  [the longest x5 23.9 us: device_body(): latents = (x_init + offset)[None] + (running - drifts)]
  transfers between devices with their start and end apart: 16 -> 0, of which waited for: 16 -> 0; matrix products, arithmetic and copies ran while one was open for 0% -> 0% of each run, Pallas kernels for 0% -> 0%
where the time goes in v1:
time: 234 us
  Pallas kernels  137 us (59%)
  blocking collectives  77.2 us (33%)
  local copies, waits for them, and re-layouts  16.2 us (7%)
    pallas_call x1, Pallas kernels, device_body(): pl.pallas_call(functools.partial(kernel, n_t, n_m), out_shape=jax.ShapeDt...  137 us
    all_gather x1, blocking collectives, device_body(): lax.all_gather(lax.all_gather(mods, 'model', axis=2, tiled=True), 'time',...  21.4 us
    all_gather x1, blocking collectives, device_body(): lax.all_gather(mods, 'model', axis=2, tiled=True)  15.3 us
    unnamed x8, local copies, waits for them, and re-layouts  15.2 us
    unnamed x1, blocking collectives  14.5 us
    all_gather x1, blocking collectives, device_body(): w2 = lax.all_gather(w_down, 'model', axis=0, tiled=True)  13.2 us
    all_gather x1, blocking collectives, device_body(): w1 = lax.all_gather(w_up, 'model', axis=1, tiled=True)  13 us

profile of v1, /device:TPU:96, one launch (start us, length us, event | category | flops | bytes accessed | tf_op | source)
XLA Modules:
  0.0 233.6 jit_solution(8313354867524181322)
XLA Ops:
  0.0 1.2 dynamic-slice
  1.9 0.9 dynamic-update-slice
  2.8 14.5 %all-reduce.h_ref = f32[128]{0:T(128)S(1)} all-reduce(f32[128]{0:T(128)S(1)} %dynamic-update-slice), channel_id=1, replica_groups=mesh['data'=1,'model'=4,'time'=8] {'time'}, use_global_device_ids=true, to_apply=%add | all-reduce | flops 128 | bytes 1024
  17.2 0.7 pad_maximum_fusion
  18.0 0.1 copy.17
  18.1 15.3 %all_gather.18 = bf16[2,16,1152]{1,0,2:T(2,128)(2,1)S(1)} all-gather(bf16[2,16,288]{1,0,2:T(2,128)(2,1)S(1)} %copy.17), channel_id=1, replica_groups=mesh['data'=1,'model'=4,'time'=8] {'model'}, dimensions={2}, use_global_device_ids=true | all-gather | bytes 92160 | tf_op jit(solution)/shard_map/all_gather | solution.py:245
  33.4 0.6 copy.18
  34.0 21.4 %all_gather.19 = bf16[2,128,1152]{2,0,1:T(2,128)(2,1)S(1)} all-gather(bf16[2,16,1152]{2,0,1:T(2,128)(2,1)S(1)} %copy.18), channel_id=1, replica_groups=mesh['data'=1,'model'=4,'time'=8] {'time'}, dimensions={1}, use_global_device_ids=true | all-gather | bytes 663552 | tf_op jit(solution)/shard_map/all_gather | solution.py:245
  55.3 0.4 convert_element_type.3
  55.7 1.1 slice_multiply_fusion
  57.0 13.0 %all_gather.16 = bf16[256,1152]{0,1:T(8,128)(2,1)S(1)} all-gather(bf16[256,288]{0,1:T(8,128)(2,1)} %param.7), channel_id=1, replica_groups=mesh['data'=1,'model'=4,'time'=8] {'model'}, dimensions={1}, use_global_device_ids=true | all-gather | bytes 737280 | tf_op jit(solution)/shard_map/all_gather | solution.py:242
  69.9 0.3 copy.19.w1_ref
  70.2 13.2 %all_gather.17.w2_ref = bf16[1152,256]{1,0:T(8,128)(2,1)S(1)} all-gather(bf16[288,256]{1,0:T(8,128)(2,1)} %param.8), channel_id=1, replica_groups=mesh['data'=1,'model'=4,'time'=8] {'model'}, dimensions={0}, use_global_device_ids=true | all-gather | bytes 737280 | tf_op jit(solution)/shard_map/all_gather | solution.py:243
  83.4 0.0 copy-start
  83.4 1.2 copy-done
  84.6 137.2 %shard_map.64 = f32[16,1024,256]{2,1,0:T(8,128)} custom-call(f32[128]{0:T(128)S(1)} %all-reduce.h_ref, f32[1024,256]{1,0:T(8,128)S(1)} %bitcast.9, bf16[256,1152]{1,0:T(8,128)(2,1)S(1)} %copy.19.w1_ref, bf16[1152,256]{1,0:T(8,128)(2,1)S(1)} %all_gather.17.w2_ref, f32[8,16,1152]{2,1,0:T(8,128)S(1)} %bitcast.8, f32[8,16,1152]{2,1,0:T(8,128)S(1)} %bitcast.7), custom_call_target="tpu_custom_call" | custom-call | tf_op jit(solution)/shard_map/pallas_call | solution.py:253
  221.8 11.8 %copy.24 = f32[16,64,16,256]{3,2,1,0:T(8,128)} copy(f32[16,64,16,256]{3,2,1,0:T(8,128)} %bitcast.10) | data formatting | bytes 33554432
  (3 shorter events, 0.1 us)
Async XLA Ops:
  83.4 1.2 copy-start

commit v2 on v0

v2 whole, which is shorter than its diff:
```python
import functools
import math

import jax
import jax.numpy as jnp
from jax import lax
from jax.experimental import pallas as pl
from jax.experimental.pallas import tpu as pltpu
from jax.sharding import PartitionSpec as P

SWEEPS = 4
ROWS = 16
STAGES = 4
F32, BF16 = jnp.float32, jnp.bfloat16
MESH_ID = pl.DeviceIdType.MESH
ROOT = math.sqrt(2.0 / math.pi)


def kernel(n_t, n_m, h_ref, x0_ref, wu_ref, wd_ref, ms_ref, mb_ref, out_ref, w1_ref, w2_ref, w1raw, w2raw, modraw, modall, hall, sc_ref, sh_ref,
           xbuf, obuf, rbuf, robuf, gbuf, stage, gws, gwr, gfs, gfr, gds, gdr, ms, mr, mxs, mxr, mds, mdr, hs, hr,
           s1s, s1r, s2s, s2r, s3s, s3r, o1s, o1r, o2s, o2r, o3s, o3r, out_sem):
    me_t = lax.axis_index('time')
    me_m = lax.axis_index('model')
    me_x, me_c = me_t // 2, me_t % 2
    n_k, n_x = xbuf.shape[0], n_t // 2
    block = xbuf.shape[2] // 2
    span = block // ROWS
    half = block // 2
    hid_dev = wu_ref.shape[1]
    hid = n_m * hid_dev
    main = hid_dev // 128 * 128
    tail = hid_dev - main
    chunks = [(lo, min(lo + 256, hid)) for lo in range(0, hid, 256)]
    up, down, far = (me_m + 1) % n_m, (me_m + n_m - 1) % n_m, (me_m + 2) % n_m
    mate = me_x * 2 + (me_c + 1) % 2
    lanes = ((0, up), (1, down))

    def hop(qx):
        return qx + (qx // 2) * (5 - 2 * qx)

    def peer(q, sign):
        return ((me_x + n_x + sign * hop(q // 2)) % n_x) * 2 + (me_c + q % 2) % 2

    def remote(src, dst, send, recv, **where):
        return pltpu.make_async_remote_copy(src_ref=src, dst_ref=dst, send_sem=send, recv_sem=recv, device_id=where, device_id_type=MESH_ID)

    tables = ((wu_ref, w1raw), (wd_ref, w2raw))

    def w_part(ref, c):
        return pl.ds(c * (ref.shape[-2] // 2), ref.shape[-2] // 2)

    def w_first(i, d, to):
        own, raw = tables[i]
        return remote(own.at[w_part(own, me_c)], raw.at[me_m, w_part(own, me_c)], gws.at[i, d], gwr.at[i, d], model=to)

    def w_forward(d, to):
        own, raw = tables[d]
        origin = (down, up)[d]
        piece = raw.at[origin, w_part(own, me_c)]
        return remote(piece, piece, gfs.at[d], gfr.at[d], model=to)

    def w_share(i, place):
        own, raw = tables[i]
        piece = raw.at[(down, up, far)[place], w_part(own, me_c)]
        return remote(piece, piece, gds.at[i, place], gdr.at[i, place], time=mate)

    def mod_first(i, place):
        return remote((ms_ref, mb_ref)[i], modraw.at[i, me_m], ms.at[i, place], mr.at[i, place], model=(up, down, far)[place])

    def mod_time(qx):
        return remote(modall.at[me_t], modall.at[me_t], mxs.at[qx], mxr.at[qx], time=((me_x + hop(qx)) % n_x) * 2 + me_c)

    def mod_share(qx):
        row = ((me_x + n_x - hop(qx)) % n_x) * 2 + me_c
        return remote(modall.at[row], modall.at[row], mds.at[qx], mdr.at[qx], time=mate)

    def h_time(q):
        return remote(hall.at[me_t], hall.at[me_t], hs.at[q], hr.at[q], time=peer(q, 1))

    barrier = pltpu.get_barrier_semaphore()

    @pl.loop(1, n_t)
    def _(q):
        pl.semaphore_signal(barrier, inc=1, device_id={'time': peer(q, 1)}, device_id_type=MESH_ID)
    for to in (up, down, far):
        pl.semaphore_signal(barrier, inc=1, device_id={'model': to}, device_id_type=MESH_ID)
    for j in range(span):
        hall[me_t, j:j + 1, :] = jnp.full((1, hall.shape[2]), h_ref[j], F32)
    w1raw[me_m] = wu_ref[...]
    w2raw[me_m] = wd_ref[...]
    modraw[0, me_m] = ms_ref[...]
    modraw[1, me_m] = mb_ref[...]
    pl.semaphore_wait(barrier, n_t + 2)

    for place in range(3):
        for i in range(2):
            mod_first(i, place).start()
    for d, to in lanes:
        for i in range(2):
            w_first(i, d, to).start()

    @pl.loop(1, n_t)
    def _(q):
        h_time(q).start()

    def joined(pieces):
        return jnp.concatenate([p[:, :main] for p in pieces] + [jnp.concatenate([p[:, main:] for p in pieces], axis=1)], axis=1)

    for place in range(3):
        for i in range(2):
            mod_first(i, place).wait_recv()
    for i in range(2):
        modall[me_t, i] = joined([modraw[i, m].astype(F32) for m in range(n_m)]).astype(BF16)
    for qx in (1, 2, 3):
        mod_time(qx).start()
    mod_share(0).start()

    for d, to in lanes:
        for i in range(2):
            w_first(i, d, to).wait_recv()
        w_forward(d, to).start()
        for i in range(2):
            w_share(i, d).start()
    for qx in (1, 2, 3):
        mod_time(qx).wait_recv()
        mod_share(qx).start()
    for d, to in lanes:
        w_forward(d, to).wait_recv()
        w_share(d, 2).start()

    @pl.loop(1, n_t)
    def _(q):
        h_time(q).wait_recv()
    for place in range(3):
        for i in range(2):
            w_share(i, place).wait_recv()
    for qx in range(n_x):
        mod_share(qx).wait_recv()
    for m in range(n_m):
        w1_ref[:, m * main:(m + 1) * main] = w1raw[m][:, :main]
        w2_ref[m * main:(m + 1) * main, :] = w2raw[m, :main, :]
        w2_ref[n_m * main + m * tail:n_m * main + (m + 1) * tail, :] = w2raw[m, main:, :]
    w1_ref[:, n_m * main:] = jnp.concatenate([w1raw[m][:, main:].astype(F32) for m in range(n_m)], axis=1).astype(BF16)

    @pl.loop(0, n_t)
    def _(t):
        sc_ref[t] = 0.5 * (1.0 + modall[t, 0].astype(F32))
        sh_ref[t] = 0.5 * modall[t, 1].astype(F32)

    def drift(x, blocks, same):
        for lo, hi in chunks:
            p = jnp.dot(x, w1_ref[:, lo:hi], preferred_element_type=F32)
            for b, tb in enumerate(blocks):
                for j in range(span):
                    at = (b * span + j) * ROWS
                    v = (p if same else p[at:at + ROWS]) * sc_ref[tb, j:j + 1, lo:hi] + sh_ref[tb, j:j + 1, lo:hi]
                    t = jnp.tanh(v * (2 * ROOT + (8 * 0.044715 * ROOT) * (v * v)))
                    gbuf[at:at + ROWS, lo:hi] = (v + v * t).astype(BF16)
        return jnp.dot(gbuf[...], w2_ref[...], preferred_element_type=F32)

    def scaled(f, b, tb, j):
        at = (b * span + j) * ROWS
        h = hall[tb, j:j + 1, :]
        return f[at:at + ROWS] * jnp.concatenate([h] * (f.shape[1] // h.shape[1]), axis=1)

    def sweep(k, number):
        x0 = x0_ref[pl.ds(((k * n_m + me_m) * n_t + me_t) * ROWS, ROWS), :]

        def body(bx, acc):
            f = drift(x0.astype(BF16) if number == 0 else xbuf[k, bx], (2 * bx, 2 * bx + 1), number == 0)
            for b in range(2):
                if number == SWEEPS - 1:
                    obuf[k, 2 * bx + b] = acc
                for j in range(span):
                    if number < SWEEPS - 1:
                        at = (b * span + j) * ROWS
                        xbuf[k, bx, at:at + ROWS, :] = (x0 + acc).astype(BF16)
                    acc = acc + scaled(f, b, 2 * bx + b, j)
            return acc

        lax.fori_loop(0, n_x, body, jnp.zeros_like(x0))

    def sub(c):
        return pl.ds(c * block, block)

    def x_copy(k, q, to, src):
        return remote(xbuf.at[k, to // 2, sub(to % 2)], rbuf.at[0, k, src // 2, sub(src % 2)], s1s.at[k, q], s1r.at[k, q], time=to)

    def x_send(k):
        @pl.loop(1, n_t)
        def _(q):
            x_copy(k, q, peer(q, 1), me_t).start()
        rbuf[0, k, me_x, sub(me_c), :] = xbuf[k, me_x, sub(me_c), :]

    def x_ring(q, k, d, to):
        src = peer(q, -1)
        i = k * n_t + q
        return remote(rbuf.at[0, k, src // 2, sub(src % 2)], rbuf.at[1 + d, k, src // 2, sub(src % 2)], s2s.at[d, i], s2r.at[d, i], model=to)

    def x_next(q, k, d, to):
        src = peer(q, -1)
        i = k * n_t + q
        part = pl.ds((src % 2) * block + d * half, half)
        return remote(rbuf.at[1 + d, k, src // 2, part], rbuf.at[3, k, src // 2, part], s3s.at[d, i], s3r.at[d, i], model=to)

    def x_row(q, k):
        @pl.when(q > 0)
        def _():
            x_copy(k, q, me_t, peer(q, -1)).wait_recv()
        for d, to in lanes:
            x_ring(q, k, d, to).start()

    def x_pass(q, k):
        for d, to in lanes:
            x_ring(q, k, d, to).wait_recv()
            x_next(q, k, d, to).start()

    def x_far(q, k):
        for d, to in lanes:
            x_next(q, k, d, to).wait_recv()

    def o_copy(k, q, to, src):
        return remote(obuf.at[k, to], robuf.at[0, k, src], o1s.at[k, q], o1r.at[k, q], time=to)

    def o_ring(k, d, to):
        return remote(robuf.at[0, k], robuf.at[1 + d, k], o2s.at[d, k], o2r.at[d, k], model=to)

    def o_next(k, d, to):
        part = pl.ds(d * n_x, n_x)
        return remote(robuf.at[1 + d, k, part], robuf.at[3, k, part], o3s.at[d, k], o3r.at[d, k], model=to)

    def o_send(k):
        @pl.loop(1, n_t)
        def _(q):
            o_copy(k, q, peer(q, 1), me_t).start()
        robuf[0, k, me_t] = obuf[k, me_t]

    def o_row(k):
        @pl.loop(1, n_t)
        def _(q):
            o_copy(k, q, me_t, peer(q, -1)).wait_recv()
        for d, to in lanes:
            o_ring(k, d, to).start()

    def o_pass(k):
        for d, to in lanes:
            o_ring(k, d, to).wait_recv()
            o_next(k, d, to).start()

    def o_far(k):
        for d, to in lanes:
            o_next(k, d, to).wait_recv()

    def out_copy(slot, row):
        return pltpu.make_async_copy(stage.at[slot], out_ref.at[:, pl.ds(row, 2 * ROWS), :], out_sem.at[slot])

    def finish(rel, pair, number):
        k, src = pair // n_x, (me_x + n_x - hop(pair % n_x)) % n_x
        origin = (me_m + (n_m - rel) + (rel // 2) * (2 * rel - 5)) % n_m
        row = (((k * n_m + origin) * n_x + src) * 2) * ROWS
        slot = number % STAGES

        @pl.when(number >= STAGES)
        def _():
            out_copy(slot, 0).wait()
        f = drift(rbuf[rel, k, src], (me_t, me_t), False)
        for b in range(2):
            x0 = x0_ref[pl.ds(row + b * ROWS, ROWS), :]
            acc = robuf[rel, k, 2 * src + b]
            for j in range(span):
                stage[slot, j, b * ROWS:(b + 1) * ROWS, :] = x0 + acc
                acc = acc + scaled(f, b, me_t, j)
        out_copy(slot, row).start()

    @pl.loop(0, n_k * SWEEPS)
    def _(step):
        k, number = step // SWEEPS, step % SWEEPS

        @pl.when(number == 0)
        def _():
            sweep(k, 0)

        @pl.when(number % (SWEEPS - 1) > 0)
        def _():
            sweep(k, 1)

        @pl.when(number == SWEEPS - 2)
        def _():
            x_send(k)

        @pl.when(number == SWEEPS - 1)
        def _():
            sweep(k, SWEEPS - 1)
            o_send(k)

        @pl.when(step == SWEEPS - 2)
        def _():
            x_row(0, 0)

        @pl.when(step == SWEEPS - 1)
        def _():
            x_row(1, 0)

        @pl.when(step == SWEEPS)
        def _():
            x_pass(0, 0)
            x_row(2, 0)
            x_row(3, 0)

        @pl.when(step == SWEEPS + 1)
        def _():
            x_pass(1, 0)
            o_row(0)
            x_row(4, 0)
            x_row(5, 0)

        @pl.when(step == SWEEPS + 2)
        def _():
            x_pass(2, 0)
            x_pass(3, 0)
            o_pass(0)

    o_far(0)

    pairs = n_k * n_x
    early, ahead = 2, 3
    for c in range(2):
        x_row(ahead % n_x * 2 + c, ahead // n_x)

    @pl.loop(0, n_m * pairs)
    def _(n):
        p, turn = (n + 1) // n_m, (n + 1) % n_m
        rel, pair = (turn + n_m - 1) % n_m, p - (n_m - turn) // n_m

        @pl.when(turn == 0)
        def _():
            @pl.when(p < pairs)
            def _():
                @pl.when(p >= early)
                def _():
                    for c in range(2):
                        x_pass(p % n_x * 2 + c, p // n_x)

            @pl.when(p < pairs - ahead)
            def _():
                for c in range(2):
                    x_row((p + ahead) % n_x * 2 + c, (p + ahead) // n_x)

            @pl.when(p == 1)
            def _():
                o_row(1)

            @pl.when(p == 3)
            def _():
                o_pass(1)

            @pl.when(p == n_x)
            def _():
                o_far(1)

            for c in range(2):
                x_far(pair % n_x * 2 + c, pair // n_x)
        finish(rel, pair, n)

    for slot in range(STAGES):
        out_copy(slot, 0).wait()

    for d, to in lanes:
        for i in range(2):
            w_first(i, d, to).wait_send()
        w_forward(d, to).wait_send()
    for place in range(3):
        for i in range(2):
            w_share(i, place).wait_send()
            mod_first(i, place).wait_send()
    for qx in range(n_x):
        if qx:
            mod_time(qx).wait_send()
        mod_share(qx).wait_send()

    @pl.loop(1, n_t)
    def _(q):
        h_time(q).wait_send()

    @pl.loop(0, n_k * n_t)
    def _(i):
        k, q = i // n_t, i % n_t

        @pl.when(q > 0)
        def _():
            x_copy(k, q, peer(q, 1), me_t).wait_send()
            o_copy(k, q, peer(q, 1), me_t).wait_send()
        for d, to in lanes:
            x_ring(q, k, d, to).wait_send()
            x_next(q, k, d, to).wait_send()
    for k in range(n_k):
        for d, to in lanes:
            o_ring(k, d, to).wait_send()
            o_next(k, d, to).wait_send()


def solution(mesh):
    n_t, n_m = mesh.shape['time'], mesh.shape['model']

    def device_body(x_init, w_up, w_down, mod_scale, mod_shift, step_size):
        (span, hid_dev), chan = mod_scale.shape, x_init.shape[-1]
        rows = x_init.shape[0] * x_init.shape[1]
        hid = n_m * hid_dev
        n_k, n_x = rows // (n_t * n_m * ROWS), n_t // 2
        vmem = pl.BlockSpec(memory_space=pltpu.VMEM)
        sem = lambda *shape: pltpu.SemaphoreType.DMA(shape)
        out = pl.pallas_call(
            functools.partial(kernel, n_t, n_m),
            out_shape=jax.ShapeDtypeStruct((span, rows, chan), F32),
            in_specs=[pl.BlockSpec(memory_space=pltpu.SMEM)] + [vmem] * 5,
            out_specs=pl.BlockSpec(memory_space=pl.ANY),
            scratch_shapes=[
                pltpu.VMEM((chan, hid), BF16),
                pltpu.VMEM((hid, chan), BF16),
                pltpu.VMEM((n_m, chan, hid_dev), BF16),
                pltpu.VMEM((n_m, hid_dev, chan), BF16),
                pltpu.VMEM((2, n_m, span, hid_dev), BF16),
                pltpu.VMEM((n_t, 2, span, hid), BF16),
                pltpu.VMEM((n_t, span, 128), F32),
                pltpu.VMEM((n_t, span, hid), F32),
                pltpu.VMEM((n_t, span, hid), F32),
                pltpu.VMEM((n_k, n_x, 2 * span * ROWS, chan), BF16),
                pltpu.VMEM((n_k, n_t, ROWS, chan), F32),
                pltpu.VMEM((n_m, n_k, n_x, 2 * span * ROWS, chan), BF16),
                pltpu.VMEM((n_m, n_k, n_t, ROWS, chan), F32),
                pltpu.VMEM((2 * span * ROWS, hid), BF16),
                pltpu.VMEM((STAGES, span, 2 * ROWS, chan), F32),
                sem(2, 2), sem(2, 2), sem(2), sem(2), sem(2, 3), sem(2, 3),
                sem(2, 3), sem(2, 3), sem(n_x), sem(n_x), sem(n_x), sem(n_x), sem(n_t), sem(n_t),
                sem(n_k, n_t), sem(n_k, n_t),
                sem(2, n_k * n_t), sem(2, n_k * n_t), sem(2, n_k * n_t), sem(2, n_k * n_t),
                sem(n_k, n_t), sem(n_k, n_t),
                sem(2, n_k), sem(2, n_k), sem(2, n_k), sem(2, n_k),
                sem(STAGES),
            ],
            compiler_params=pltpu.CompilerParams(collective_id=0, has_side_effects=True, vmem_limit_bytes=48 << 20),
        )(step_size, x_init.reshape(rows, chan), w_up, w_down, mod_scale, mod_shift)
        return out.reshape((span,) + x_init.shape)

    return jax.shard_map(device_body, mesh=mesh, in_specs=(P('data', None, None), P(None, 'model'), P('model', None), P('time', 'model'), P('time', 'model'), P('time')), out_specs=P('time', 'data', None, None), check_vma=False)
```

time: 1630 us -> 143 us (0.09)
  waiting for transfers between devices: 1340 us -> 0 us
  Pallas kernels: 0 us -> 125 us
  starting transfers between devices: 93.4 us -> 0 us
  other arithmetic: 86.7 us -> 0 us
  matrix products: 85.5 us -> 0 us
    psum x4 -> x0, waiting for transfers between devices: 1170 us -> none  [device_body(): drifts = step_col * lax.psum(part_drift, 'model')]
    ppermute x12 -> x0, waiting for transfers between devices: 177 us -> none  [device_body(): scan_acc = scan_acc + lax.ppermute(scan_acc, 'time', perm_pairs)]
    pallas_call x0 -> x1, Pallas kernels: none -> 125 us  [device_body(): pl.pallas_call(functools.partial(kernel, n_t, n_m), out_shape=jax.ShapeDt...]
    ppermute x12 -> x0, starting transfers between devices: 93.2 us -> none  [device_body(): scan_acc = scan_acc + lax.ppermute(scan_acc, 'time', perm_pairs)]
    dot_general x4 -> x0, matrix products: 85.5 us -> none  [local_drift(): jnp.einsum('tbnd,dc->tbnc', hidden.astype(jnp.bfloat16), w_down, preferre...]
    another operation x4 -> x0, other arithmetic: 53.4 us -> none  [device_body(): running = jnp.cumsum(drifts, axis=0)]
    add x14 -> x0, other arithmetic: 31.2 us -> none  [the longest x5 23.9 us: device_body(): latents = (x_init + offset)[None] + (running - drifts)]
    unnamed x8 -> x12, local copies, waits for them, and re-layouts: 0.02 us -> 17 us
  transfers between devices with their start and end apart: 16 -> 0, of which waited for: 16 -> 0; matrix products, arithmetic and copies ran while one was open for 0% -> 0% of each run, Pallas kernels for 0% -> 0%
where the time goes in v2:
time: 143 us; the launch traced here: 142 us
  Pallas kernels  125 us (87%)
  local copies, waits for them, and re-layouts  17 us (12%)
    pallas_call x1, Pallas kernels, device_body(): pl.pallas_call(functools.partial(kernel, n_t, n_m), out_shape=jax.ShapeDt...  125 us
    unnamed x12, local copies, waits for them, and re-layouts  17 us

profile of v2, /device:TPU:96, one launch (start us, length us, event | category | flops | bytes accessed | tf_op | source)
XLA Modules:
  0.0 141.9 jit_solution(7815702324615015695)
XLA Ops:
  0.0 1.1 copy.7.wu_ref
  1.1 0.0 copy-start
  1.1 1.2 copy-done
  2.3 0.0 copy-start.1
  2.3 0.9 copy-done.1
  3.2 0.0 copy-start.2
  3.2 0.7 copy-done.2
  3.9 0.0 copy-start.3
  3.9 0.7 copy-done.3
  4.6 0.0 copy-start.4
  4.6 0.7 copy-done.4
  5.3 124.9 %shard_map.64 = f32[16,1024,256]{2,1,0:T(8,128)} custom-call(f32[16]{0:T(128)S(1)} %copy-done.4, f32[1024,256]{1,0:T(8,128)S(1)} %bitcast.2, bf16[256,288]{1,0:T(8,128)(2,1)S(1)} %copy.7.wu_ref, bf16[288,256]{1,0:T(8,128)(2,1)S(1)} %copy-done.1, bf16[16,288]{1,0:T(8,128)(2,1)S(1)} %copy-done.2, bf16[16,288]{1,0:T(8,128)(2,1)S(1)} %copy-done.3), custom_call_target="tpu_custom_call" | custom-call | tf_op jit(solution)/shard_map/pallas_call | solution.py:412
  130.2 11.8 %copy.9 = f32[16,64,16,256]{3,2,1,0:T(8,128)} copy(f32[16,64,16,256]{3,2,1,0:T(8,128)} %bitcast.3) | data formatting | bytes 33554432
Async XLA Ops:
  1.1 1.2 copy-start
  2.3 0.9 copy-start.1
  3.2 0.7 copy-start.2
  3.9 0.7 copy-start.3
  4.6 0.7 copy-start.4

commit v3 on v2

--- a/solution.py
+++ b/solution.py
@@ -9,6 +9,7 @@
 from jax.sharding import PartitionSpec as P
 
 SWEEPS = 4
+VMEM_BYTES = 67043328
 ROWS = 16
 STAGES = 4
 F32, BF16 = jnp.float32, jnp.bfloat16
@@ -16,9 +17,9 @@
 ROOT = math.sqrt(2.0 / math.pi)
 
 
-def kernel(n_t, n_m, h_ref, x0_ref, wu_ref, wd_ref, ms_ref, mb_ref, out_ref, w1_ref, w2_ref, w1raw, w2raw, modraw, modall, hall, sc_ref, sh_ref,
-           xbuf, obuf, rbuf, robuf, gbuf, stage, gws, gwr, gfs, gfr, gds, gdr, ms, mr, mxs, mxr, mds, mdr, hs, hr,
-           s1s, s1r, s2s, s2r, s3s, s3r, o1s, o1r, o2s, o2r, o3s, o3r, out_sem):
+def kernel(n_t, n_m, h_hbm, x0_hbm, wu_hbm, wd_hbm, ms_hbm, mb_hbm, out_ref, h_ref, x0_ref, w1_ref, w1t_ref, w2_ref, modraw, modall, hall, sc_ref, sh_ref,
+           xbuf, obuf, rbuf, robuf, gbuf, own_sem, gws, gwr, gfs, gfr, gds, gdr, ms, mr, mxs, mxr, mds, mdr, hs, hr,
+           s1s, s1r, s2s, s2r, s3s, s3r, o1s, o1r, o2s, o2r, o3s, o3r):
     me_t = lax.axis_index('time')
     me_m = lax.axis_index('model')
     me_x, me_c = me_t // 2, me_t % 2
@@ -26,10 +27,8 @@
     block = xbuf.shape[2] // 2
     span = block // ROWS
     half = block // 2
-    hid_dev = wu_ref.shape[1]
+    hid_dev = modraw.shape[3]
     hid = n_m * hid_dev
-    main = hid_dev // 128 * 128
-    tail = hid_dev - main
     chunks = [(lo, min(lo + 256, hid)) for lo in range(0, hid, 256)]
     up, down, far = (me_m + 1) % n_m, (me_m + n_m - 1) % n_m, (me_m + 2) % n_m
     mate = me_x * 2 + (me_c + 1) % 2
@@ -44,28 +43,26 @@
     def remote(src, dst, send, recv, **where):
         return pltpu.make_async_remote_copy(src_ref=src, dst_ref=dst, send_sem=send, recv_sem=recv, device_id=where, device_id_type=MESH_ID)
 
-    tables = ((wu_ref, w1raw), (wd_ref, w2raw))
-
-    def w_part(ref, c):
-        return pl.ds(c * (ref.shape[-2] // 2), ref.shape[-2] // 2)
+    tables = (w1t_ref, w2_ref)
+
+    def w_rows(origin, c):
+        rows = hid_dev // 2
+        return pl.ds(pl.multiple_of(origin * hid_dev + c * rows, 16), rows)
 
     def w_first(i, d, to):
-        own, raw = tables[i]
-        return remote(own.at[w_part(own, me_c)], raw.at[me_m, w_part(own, me_c)], gws.at[i, d], gwr.at[i, d], model=to)
+        piece = tables[i].at[w_rows(me_m, me_c)]
+        return remote(piece, piece, gws.at[i, d], gwr.at[i, d], model=to)
 
     def w_forward(d, to):
-        own, raw = tables[d]
-        origin = (down, up)[d]
-        piece = raw.at[origin, w_part(own, me_c)]
+        piece = tables[d].at[w_rows((down, up)[d], me_c)]
         return remote(piece, piece, gfs.at[d], gfr.at[d], model=to)
 
     def w_share(i, place):
-        own, raw = tables[i]
-        piece = raw.at[(down, up, far)[place], w_part(own, me_c)]
+        piece = tables[i].at[w_rows((down, up, far)[place], me_c)]
         return remote(piece, piece, gds.at[i, place], gdr.at[i, place], time=mate)
 
     def mod_first(i, place):
-        return remote((ms_ref, mb_ref)[i], modraw.at[i, me_m], ms.at[i, place], mr.at[i, place], model=(up, down, far)[place])
+        return remote(modraw.at[i, me_m], modraw.at[i, me_m], ms.at[i, place], mr.at[i, place], model=(up, down, far)[place])
 
     def mod_time(qx):
         return remote(modall.at[me_t], modall.at[me_t], mxs.at[qx], mxr.at[qx], time=((me_x + hop(qx)) % n_x) * 2 + me_c)
@@ -77,6 +74,11 @@
     def h_time(q):
         return remote(hall.at[me_t], hall.at[me_t], hs.at[q], hr.at[q], time=peer(q, 1))
 
+    mine = pl.ds(pl.multiple_of(me_m * hid_dev, 16), hid_dev)
+    own = [pltpu.make_async_copy(src, dst, own_sem.at[i]) for i, (src, dst) in enumerate((
+        (ms_hbm, modraw.at[0, me_m]), (mb_hbm, modraw.at[1, me_m]), (wu_hbm, w1t_ref.at[mine]), (wd_hbm, w2_ref.at[mine]), (h_hbm, h_ref), (x0_hbm, x0_ref)))]
+    for copy in own:
+        copy.start()
     barrier = pltpu.get_barrier_semaphore()
 
     @pl.loop(1, n_t)
@@ -84,43 +86,39 @@
         pl.semaphore_signal(barrier, inc=1, device_id={'time': peer(q, 1)}, device_id_type=MESH_ID)
     for to in (up, down, far):
         pl.semaphore_signal(barrier, inc=1, device_id={'model': to}, device_id_type=MESH_ID)
+    for copy in own:
+        copy.wait()
     for j in range(span):
         hall[me_t, j:j + 1, :] = jnp.full((1, hall.shape[2]), h_ref[j], F32)
-    w1raw[me_m] = wu_ref[...]
-    w2raw[me_m] = wd_ref[...]
-    modraw[0, me_m] = ms_ref[...]
-    modraw[1, me_m] = mb_ref[...]
     pl.semaphore_wait(barrier, n_t + 2)
 
     for place in range(3):
         for i in range(2):
             mod_first(i, place).start()
     for d, to in lanes:
-        for i in range(2):
+        for i in (d, 1 - d):
             w_first(i, d, to).start()
 
     @pl.loop(1, n_t)
     def _(q):
         h_time(q).start()
-
-    def joined(pieces):
-        return jnp.concatenate([p[:, :main] for p in pieces] + [jnp.concatenate([p[:, main:] for p in pieces], axis=1)], axis=1)
 
     for place in range(3):
         for i in range(2):
             mod_first(i, place).wait_recv()
     for i in range(2):
-        modall[me_t, i] = joined([modraw[i, m].astype(F32) for m in range(n_m)]).astype(BF16)
+        modall[me_t, i] = jnp.concatenate([modraw[i, m].astype(F32) for m in range(n_m)], axis=1).astype(BF16)
     for qx in (1, 2, 3):
         mod_time(qx).start()
     mod_share(0).start()
 
     for d, to in lanes:
-        for i in range(2):
-            w_first(i, d, to).wait_recv()
+        w_first(d, d, to).wait_recv()
         w_forward(d, to).start()
-        for i in range(2):
-            w_share(i, d).start()
+        w_share(d, d).start()
+    for d, to in lanes:
+        w_first(1 - d, d, to).wait_recv()
+        w_share(1 - d, d).start()
     for qx in (1, 2, 3):
         mod_time(qx).wait_recv()
         mod_share(qx).start()
@@ -131,21 +129,19 @@
     @pl.loop(1, n_t)
     def _(q):
         h_time(q).wait_recv()
-    for place in range(3):
-        for i in range(2):
-            w_share(i, place).wait_recv()
     for qx in range(n_x):
         mod_share(qx).wait_recv()
-    for m in range(n_m):
-        w1_ref[:, m * main:(m + 1) * main] = w1raw[m][:, :main]
-        w2_ref[m * main:(m + 1) * main, :] = w2raw[m, :main, :]
-        w2_ref[n_m * main + m * tail:n_m * main + (m + 1) * tail, :] = w2raw[m, main:, :]
-    w1_ref[:, n_m * main:] = jnp.concatenate([w1raw[m][:, main:].astype(F32) for m in range(n_m)], axis=1).astype(BF16)
 
     @pl.loop(0, n_t)
     def _(t):
         sc_ref[t] = 0.5 * (1.0 + modall[t, 0].astype(F32))
         sh_ref[t] = 0.5 * modall[t, 1].astype(F32)
+
+    for place in range(3):
+        for i in range(2):
+            w_share(i, place).wait_recv()
+    for lo in range(0, hid, 128):
+        w1_ref[:, lo:lo + 128] = w1t_ref[lo:lo + 128, :].T
 
     def drift(x, blocks, same):
         for lo, hi in chunks:
@@ -251,26 +247,17 @@
         for d, to in lanes:
             o_next(k, d, to).wait_recv()
 
-    def out_copy(slot, row):
-        return pltpu.make_async_copy(stage.at[slot], out_ref.at[:, pl.ds(row, 2 * ROWS), :], out_sem.at[slot])
-
-    def finish(rel, pair, number):
+    def finish(rel, pair):
         k, src = pair // n_x, (me_x + n_x - hop(pair % n_x)) % n_x
         origin = (me_m + (n_m - rel) + (rel // 2) * (2 * rel - 5)) % n_m
-        row = (((k * n_m + origin) * n_x + src) * 2) * ROWS
-        slot = number % STAGES
-
-        @pl.when(number >= STAGES)
-        def _():
-            out_copy(slot, 0).wait()
+        row = pl.multiple_of((((k * n_m + origin) * n_x + src) * 2) * ROWS, 2 * ROWS)
         f = drift(rbuf[rel, k, src], (me_t, me_t), False)
         for b in range(2):
             x0 = x0_ref[pl.ds(row + b * ROWS, ROWS), :]
             acc = robuf[rel, k, 2 * src + b]
             for j in range(span):
-                stage[slot, j, b * ROWS:(b + 1) * ROWS, :] = x0 + acc
+                out_ref[j, pl.ds(row + b * ROWS, ROWS), :] = x0 + acc
                 acc = acc + scaled(f, b, me_t, j)
-        out_copy(slot, row).start()
 
     @pl.loop(0, n_k * SWEEPS)
     def _(step):
@@ -360,10 +347,7 @@
 
             for c in range(2):
                 x_far(pair % n_x * 2 + c, pair // n_x)
-        finish(rel, pair, n)
-
-    for slot in range(STAGES):
-        out_copy(slot, 0).wait()
+        finish(rel, pair)
 
     for d, to in lanes:
         for i in range(2):
@@ -399,6 +383,15 @@
             o_next(k, d, to).wait_send()
 
 
+def drain(n, src_ref, out_ref, sems):
+    size = out_ref.shape[0] // n
+    copies = [pltpu.make_async_copy(src_ref.at[pl.ds(i * size, size)], out_ref.at[pl.ds(i * size, size)], sems.at[i]) for i in range(n)]
+    for copy in copies:
+        copy.start()
+    for copy in copies:
+        copy.wait()
+
+
 def solution(mesh):
     n_t, n_m = mesh.shape['time'], mesh.shape['model']
 
@@ -409,16 +402,18 @@
         n_k, n_x = rows // (n_t * n_m * ROWS), n_t // 2
         vmem = pl.BlockSpec(memory_space=pltpu.VMEM)
         sem = lambda *shape: pltpu.SemaphoreType.DMA(shape)
+        hbm = pl.BlockSpec(memory_space=pltpu.HBM)
         out = pl.pallas_call(
             functools.partial(kernel, n_t, n_m),
-            out_shape=jax.ShapeDtypeStruct((span, rows, chan), F32),
-            in_specs=[pl.BlockSpec(memory_space=pltpu.SMEM)] + [vmem] * 5,
-            out_specs=pl.BlockSpec(memory_space=pl.ANY),
+            out_shape=pltpu.VMEM((span, rows, chan), F32),
+            in_specs=[hbm] * 6,
+            out_specs=vmem,
             scratch_shapes=[
+                pltpu.SMEM((span,), F32),
+                pltpu.VMEM((rows, chan), F32),
                 pltpu.VMEM((chan, hid), BF16),
                 pltpu.VMEM((hid, chan), BF16),
-                pltpu.VMEM((n_m, chan, hid_dev), BF16),
-                pltpu.VMEM((n_m, hid_dev, chan), BF16),
+                pltpu.VMEM((hid, chan), BF16),
                 pltpu.VMEM((2, n_m, span, hid_dev), BF16),
                 pltpu.VMEM((n_t, 2, span, hid), BF16),
                 pltpu.VMEM((n_t, span, 128), F32),
@@ -429,17 +424,24 @@
                 pltpu.VMEM((n_m, n_k, n_x, 2 * span * ROWS, chan), BF16),
                 pltpu.VMEM((n_m, n_k, n_t, ROWS, chan), F32),
                 pltpu.VMEM((2 * span * ROWS, hid), BF16),
-                pltpu.VMEM((STAGES, span, 2 * ROWS, chan), F32),
+                sem(6),
                 sem(2, 2), sem(2, 2), sem(2), sem(2), sem(2, 3), sem(2, 3),
                 sem(2, 3), sem(2, 3), sem(n_x), sem(n_x), sem(n_x), sem(n_x), sem(n_t), sem(n_t),
                 sem(n_k, n_t), sem(n_k, n_t),
                 sem(2, n_k * n_t), sem(2, n_k * n_t), sem(2, n_k * n_t), sem(2, n_k * n_t),
                 sem(n_k, n_t), sem(n_k, n_t),
                 sem(2, n_k), sem(2, n_k), sem(2, n_k), sem(2, n_k),
-                sem(STAGES),
             ],
-            compiler_params=pltpu.CompilerParams(collective_id=0, has_side_effects=True, vmem_limit_bytes=48 << 20),
-        )(step_size, x_init.reshape(rows, chan), w_up, w_down, mod_scale, mod_shift)
+            compiler_params=pltpu.CompilerParams(collective_id=0, has_side_effects=True, vmem_limit_bytes=VMEM_BYTES - 4 * span * rows * chan),
+        )(step_size, x_init.reshape(rows, chan), w_up.T, w_down, mod_scale, mod_shift)
+        out = pl.pallas_call(
+            functools.partial(drain, STAGES),
+            out_shape=jax.ShapeDtypeStruct((span, rows, chan), F32),
+            in_specs=[vmem],
+            out_specs=hbm,
+            scratch_shapes=[sem(STAGES)],
+            compiler_params=pltpu.CompilerParams(vmem_limit_bytes=2 << 20),
+        )(out)
         return out.reshape((span,) + x_init.shape)
 
     return jax.shard_map(device_body, mesh=mesh, in_specs=(P('data', None, None), P(None, 'model'), P('model', None), P('time', 'model'), P('time', 'model'), P('time')), out_specs=P('time', 'data', None, None), check_vma=False)

time: 143 us -> 128 us (0.90)
  local copies, waits for them, and re-layouts: 17 us -> 0 us
  Pallas kernels: 125 us -> 127 us
    unnamed x12 -> x0, local copies, waits for them, and re-layouts: 17 us -> none
    pallas_call x1 -> x2, Pallas kernels: 125 us -> 127 us  [the longest x1 121 us: device_body(): pl.pallas_call(functools.partial(kernel, n_t, n_m), out_shape=pltpu.VMEM(...]
where the time goes in v3:
time: 128 us; the launch traced here: 127 us
  Pallas kernels  127 us (99%)
    pallas_call x1, Pallas kernels, device_body(): pl.pallas_call(functools.partial(kernel, n_t, n_m), out_shape=pltpu.VMEM(...  121 us
    pallas_call x1, Pallas kernels, device_body(): pl.pallas_call(functools.partial(drain, STAGES), out_shape=jax.ShapeDtype...  5.95 us

profile of v3, /device:TPU:96, one launch (start us, length us, event | category | flops | bytes accessed | tf_op | source)
XLA Modules:
  0.0 127.2 jit_solution(16291721098190694899)
XLA Ops:
  0.0 121.2 %shard_map.64.src_ref = f32[16,1024,256]{2,1,0:T(8,128)S(1)} custom-call(f32[16]{0:T(128)} %h_hbm.1, f32[1024,256]{1,0:T(8,128)} %bitcast.3, bf16[288,256]{1,0:T(8,128)(2,1)} %bitcast.4, bf16[288,256]{1,0:T(8,128)(2,1)} %wd_hbm.1, bf16[16,288]{1,0:T(8,128)(2,1)} %ms_hbm.1, bf16[16,288]{1,0:T(8,128)(2,1)} %mb_hbm.1), custom_call_target="tpu_custom_call" | custom-call | tf_op jit(solution)/shard_map/pallas_call | solution.py:406
  121.2 6.0 %shard_map.65 = f32[16,1024,256]{2,1,0:T(8,128)} custom-call(f32[16,1024,256]{2,1,0:T(8,128)S(1)} %shard_map.64.src_ref), custom_call_target="tpu_custom_call" | custom-call | tf_op jit(solution)/shard_map/pallas_call | solution.py:437

commit v4 on v3

--- a/solution.py
+++ b/solution.py
@@ -23,13 +23,14 @@
     me_t = lax.axis_index('time')
     me_m = lax.axis_index('model')
     me_x, me_c = me_t // 2, me_t % 2
-    n_k, n_x = xbuf.shape[0], n_t // 2
+    n_g, n_x = obuf.shape[0], n_t // 2
+    n_k = robuf.shape[1]
     block = xbuf.shape[2] // 2
     span = block // ROWS
     half = block // 2
     hid_dev = modraw.shape[3]
     hid = n_m * hid_dev
-    chunks = [(lo, min(lo + 256, hid)) for lo in range(0, hid, 256)]
+    chunks = ((0, 512), (512, hid))
     up, down, far = (me_m + 1) % n_m, (me_m + n_m - 1) % n_m, (me_m + 2) % n_m
     mate = me_x * 2 + (me_c + 1) % 2
     lanes = ((0, up), (1, down))
@@ -73,6 +74,11 @@
 
     def h_time(q):
         return remote(hall.at[me_t], hall.at[me_t], hs.at[q], hr.at[q], time=peer(q, 1))
+
+    def x0_of(g):
+        origin = (me_m + 2 * (g // 2)) % n_m
+        row = (((g + 1) // 2 * n_m + origin) * n_t + me_t) * ROWS
+        return x0_ref[pl.ds(pl.multiple_of(row, ROWS), ROWS), :]
 
     mine = pl.ds(pl.multiple_of(me_m * hid_dev, 16), hid_dev)
     own = [pltpu.make_async_copy(src, dst, own_sem.at[i]) for i, (src, dst) in enumerate((
@@ -103,6 +109,10 @@
     def _(q):
         h_time(q).start()
 
+    @pl.loop(0, n_g * n_x)
+    def _(i):
+        xbuf[i // n_x, i % n_x] = jnp.concatenate([x0_of(i // n_x).astype(BF16)] * (2 * span), axis=0)
+
     for place in range(3):
         for i in range(2):
             mod_first(i, place).wait_recv()
@@ -143,50 +153,61 @@
     for lo in range(0, hid, 128):
         w1_ref[:, lo:lo + 128] = w1t_ref[lo:lo + 128, :].T
 
-    def drift(x, blocks, same):
+    def lift(slot, x, blocks):
         for lo, hi in chunks:
             p = jnp.dot(x, w1_ref[:, lo:hi], preferred_element_type=F32)
             for b, tb in enumerate(blocks):
                 for j in range(span):
                     at = (b * span + j) * ROWS
-                    v = (p if same else p[at:at + ROWS]) * sc_ref[tb, j:j + 1, lo:hi] + sh_ref[tb, j:j + 1, lo:hi]
+                    v = p[at:at + ROWS] * sc_ref[tb, j:j + 1, lo:hi] + sh_ref[tb, j:j + 1, lo:hi]
                     t = jnp.tanh(v * (2 * ROOT + (8 * 0.044715 * ROOT) * (v * v)))
-                    gbuf[at:at + ROWS, lo:hi] = (v + v * t).astype(BF16)
-        return jnp.dot(gbuf[...], w2_ref[...], preferred_element_type=F32)
+                    gbuf[slot, at:at + ROWS, lo:hi] = (v + v * t).astype(BF16)
+
+    def lower(slot):
+        return jnp.dot(gbuf[slot], w2_ref[...], preferred_element_type=F32)
 
     def scaled(f, b, tb, j):
         at = (b * span + j) * ROWS
         h = hall[tb, j:j + 1, :]
         return f[at:at + ROWS] * jnp.concatenate([h] * (f.shape[1] // h.shape[1]), axis=1)
 
-    def sweep(k, number):
-        x0 = x0_ref[pl.ds(((k * n_m + me_m) * n_t + me_t) * ROWS, ROWS), :]
-
-        def body(bx, acc):
-            f = drift(x0.astype(BF16) if number == 0 else xbuf[k, bx], (2 * bx, 2 * bx + 1), number == 0)
+    def place_of(g):
+        return 3 * (g // 2), (g + 1) // 2
+
+    def sweep(g, number):
+        x0 = x0_of(g)
+        to = g + number // (SWEEPS - 1) * (n_g - g)
+        acc = jnp.zeros_like(x0)
+        lift(0, xbuf[g, 0], (0, 1))
+        for bx in range(n_x):
+            if bx + 1 < n_x:
+                lift((bx + 1) % 2, xbuf[g, bx + 1], (2 * bx + 2, 2 * bx + 3))
+            f = lower(bx % 2)
             for b in range(2):
-                if number == SWEEPS - 1:
-                    obuf[k, 2 * bx + b] = acc
+                obuf[g, 2 * bx + b] = acc
                 for j in range(span):
-                    if number < SWEEPS - 1:
-                        at = (b * span + j) * ROWS
-                        xbuf[k, bx, at:at + ROWS, :] = (x0 + acc).astype(BF16)
+                    at = (b * span + j) * ROWS
+                    xbuf[to, bx, at:at + ROWS, :] = (x0 + acc).astype(BF16)
                     acc = acc + scaled(f, b, 2 * bx + b, j)
-            return acc
-
-        lax.fori_loop(0, n_x, body, jnp.zeros_like(x0))
 
     def sub(c):
         return pl.ds(c * block, block)
 
-    def x_copy(k, q, to, src):
-        return remote(xbuf.at[k, to // 2, sub(to % 2)], rbuf.at[0, k, src // 2, sub(src % 2)], s1s.at[k, q], s1r.at[k, q], time=to)
-
-    def x_send(k):
+    def x_copy(g, q, to, src):
+        rel, k = place_of(g)
+        return remote(xbuf.at[g, to // 2, sub(to % 2)], rbuf.at[rel, k, src // 2, sub(src % 2)], s1s.at[g, q], s1r.at[g, q], time=to)
+
+    def x_send(g):
         @pl.loop(1, n_t)
         def _(q):
-            x_copy(k, q, peer(q, 1), me_t).start()
-        rbuf[0, k, me_x, sub(me_c), :] = xbuf[k, me_x, sub(me_c), :]
+            x_copy(g, q, peer(q, 1), me_t).start()
+        rel, k = place_of(g)
+        rbuf[rel, k, me_x, sub(me_c), :] = xbuf[g, me_x, sub(me_c), :]
+
+    def x_come(g, q):
+        @pl.when(q > 0)
+        def _():
+            x_copy(g, q, me_t, peer(q, -1)).wait_recv()
 
     def x_ring(q, k, d, to):
         src = peer(q, -1)
@@ -200,9 +221,7 @@
         return remote(rbuf.at[1 + d, k, src // 2, part], rbuf.at[3, k, src // 2, part], s3s.at[d, i], s3r.at[d, i], model=to)
 
     def x_row(q, k):
-        @pl.when(q > 0)
-        def _():
-            x_copy(k, q, me_t, peer(q, -1)).wait_recv()
+        x_come(k, q)
         for d, to in lanes:
             x_ring(q, k, d, to).start()
 
@@ -215,8 +234,9 @@
         for d, to in lanes:
             x_next(q, k, d, to).wait_recv()
 
-    def o_copy(k, q, to, src):
-        return remote(obuf.at[k, to], robuf.at[0, k, src], o1s.at[k, q], o1r.at[k, q], time=to)
+    def o_copy(g, q, to, src):
+        rel, k = place_of(g)
+        return remote(obuf.at[g, to], robuf.at[rel, k, src], o1s.at[g, q], o1r.at[g, q], time=to)
 
     def o_ring(k, d, to):
         return remote(robuf.at[0, k], robuf.at[1 + d, k], o2s.at[d, k], o2r.at[d, k], model=to)
@@ -225,16 +245,20 @@
         part = pl.ds(d * n_x, n_x)
         return remote(robuf.at[1 + d, k, part], robuf.at[3, k, part], o3s.at[d, k], o3r.at[d, k], model=to)
 
-    def o_send(k):
+    def o_send(g):
         @pl.loop(1, n_t)
         def _(q):
-            o_copy(k, q, peer(q, 1), me_t).start()
-        robuf[0, k, me_t] = obuf[k, me_t]
-
-    def o_row(k):
+            o_copy(g, q, peer(q, 1), me_t).start()
+        rel, k = place_of(g)
+        robuf[rel, k, me_t] = obuf[g, me_t]
+
+    def o_come(g):
         @pl.loop(1, n_t)
         def _(q):
-            o_copy(k, q, me_t, peer(q, -1)).wait_recv()
+            o_copy(g, q, me_t, peer(q, -1)).wait_recv()
+
+    def o_row(k):
+        o_come(k)
         for d, to in lanes:
             o_ring(k, d, to).start()
 
@@ -247,107 +271,110 @@
         for d, to in lanes:
             o_next(k, d, to).wait_recv()
 
-    def finish(rel, pair):
+    def finish(rels, pair):
         k, src = pair // n_x, (me_x + n_x - hop(pair % n_x)) % n_x
-        origin = (me_m + (n_m - rel) + (rel // 2) * (2 * rel - 5)) % n_m
-        row = pl.multiple_of((((k * n_m + origin) * n_x + src) * 2) * ROWS, 2 * ROWS)
-        f = drift(rbuf[rel, k, src], (me_t, me_t), False)
-        for b in range(2):
-            x0 = x0_ref[pl.ds(row + b * ROWS, ROWS), :]
-            acc = robuf[rel, k, 2 * src + b]
-            for j in range(span):
-                out_ref[j, pl.ds(row + b * ROWS, ROWS), :] = x0 + acc
-                acc = acc + scaled(f, b, me_t, j)
-
-    @pl.loop(0, n_k * SWEEPS)
+        for slot, rel in enumerate(rels):
+            lift(slot, rbuf[rel, k, src], (me_t, me_t))
+        for slot, rel in enumerate(rels):
+            origin = (me_m + (n_m - rel) + (rel // 2) * (2 * rel - 5)) % n_m
+            row = pl.multiple_of((((k * n_m + origin) * n_x + src) * 2) * ROWS, 2 * ROWS)
+            f = lower(slot)
+            for b in range(2):
+                x0 = x0_ref[pl.ds(row + b * ROWS, ROWS), :]
+                acc = robuf[rel, k, 2 * src + b]
+                for j in range(span):
+                    out_ref[j, pl.ds(row + b * ROWS, ROWS), :] = x0 + acc
+                    acc = acc + scaled(f, b, me_t, j)
+
+    def row_at(i):
+        x_row(i % n_t, i // n_t)
+
+    @pl.loop(0, n_g * SWEEPS)
     def _(step):
-        k, number = step // SWEEPS, step % SWEEPS
-
-        @pl.when(number == 0)
-        def _():
-            sweep(k, 0)
-
-        @pl.when(number % (SWEEPS - 1) > 0)
-        def _():
-            sweep(k, 1)
+        g, number = step // SWEEPS, step % SWEEPS
+        sweep(g, number)
 
         @pl.when(number == SWEEPS - 2)
         def _():
-            x_send(k)
+            x_send(g)
 
         @pl.when(number == SWEEPS - 1)
         def _():
-            sweep(k, SWEEPS - 1)
-            o_send(k)
-
-        @pl.when(step == SWEEPS - 2)
-        def _():
-            x_row(0, 0)
-
-        @pl.when(step == SWEEPS - 1)
-        def _():
-            x_row(1, 0)
-
-        @pl.when(step == SWEEPS)
-        def _():
-            x_pass(0, 0)
-            x_row(2, 0)
-            x_row(3, 0)
-
-        @pl.when(step == SWEEPS + 1)
-        def _():
-            x_pass(1, 0)
+            o_send(g)
+
+        @pl.when(step == 2)
+        def _():
+            row_at(0)
+
+        @pl.when(step == 3)
+        def _():
+            row_at(1)
+
+        @pl.when(step == 4)
+        def _():
+            row_at(2)
+
+        @pl.when(step > 3)
+        def _():
+            row_at(step - 1)
+
+        @pl.when(step > 4)
+        def _():
+            x_pass(step - 5, 0)
+
+        @pl.when(step == 5)
+        def _():
             o_row(0)
-            x_row(4, 0)
-            x_row(5, 0)
-
-        @pl.when(step == SWEEPS + 2)
-        def _():
-            x_pass(2, 0)
-            x_pass(3, 0)
+
+        @pl.when(step == 7)
+        def _():
             o_pass(0)
 
+        @pl.when(step == 9)
+        def _():
+            o_row(1)
+
+    passed = n_g * SWEEPS - 5
+    rowed = n_g * SWEEPS - 1
+    for q in range(passed, n_t):
+        x_pass(q, 0)
     o_far(0)
 
-    pairs = n_k * n_x
-    early, ahead = 2, 3
-    for c in range(2):
-        x_row(ahead % n_x * 2 + c, ahead // n_x)
-
-    @pl.loop(0, n_m * pairs)
-    def _(n):
-        p, turn = (n + 1) // n_m, (n + 1) % n_m
-        rel, pair = (turn + n_m - 1) % n_m, p - (n_m - turn) // n_m
-
-        @pl.when(turn == 0)
-        def _():
-            @pl.when(p < pairs)
+    @pl.loop(0, n_k * n_x * 2)
+    def _(i):
+        pair, part = i // 2, i % 2
+        k, at = pair // n_x, pair % n_x * 2
+
+        @pl.when(part == 0)
+        def _():
+            @pl.when(pair + rowed < n_k * n_t)
             def _():
-                @pl.when(p >= early)
-                def _():
-                    for c in range(2):
-                        x_pass(p % n_x * 2 + c, p // n_x)
-
-            @pl.when(p < pairs - ahead)
+                row_at(pair + rowed)
+
+            @pl.when(pair == n_x)
+            def _():
+                for d, to in lanes:
+                    o_ring(1, d, to).wait_recv()
+                o_come(2)
+
+            @pl.when(k == 1)
             def _():
                 for c in range(2):
-                    x_row((p + ahead) % n_x * 2 + c, (p + ahead) // n_x)
-
-            @pl.when(p == 1)
+                    x_ring(at + c, 1, 0, up).wait_recv()
+
+        @pl.when(part == 1)
+        def _():
+            @pl.when(k == 0)
             def _():
-                o_row(1)
-
-            @pl.when(p == 3)
+                for c in range(2):
+                    x_far(at + c, 0)
+
+            @pl.when(k == 1)
             def _():
-                o_pass(1)
-
-            @pl.when(p == n_x)
-            def _():
-                o_far(1)
-
-            for c in range(2):
-                x_far(pair % n_x * 2 + c, pair // n_x)
-        finish(rel, pair)
+                for c in range(2):
+                    x_ring(at + c, 1, 1, down).wait_recv()
+                    x_come(2, at + c)
+        finish((2 * part, 2 * part + 1), pair)
 
     for d, to in lanes:
         for i in range(2):
@@ -366,21 +393,28 @@
     def _(q):
         h_time(q).wait_send()
 
+    @pl.loop(0, n_g * n_t)
+    def _(i):
+        g, q = i // n_t, i % n_t
+
+        @pl.when(q > 0)
+        def _():
+            x_copy(g, q, peer(q, 1), me_t).wait_send()
+            o_copy(g, q, peer(q, 1), me_t).wait_send()
+
     @pl.loop(0, n_k * n_t)
     def _(i):
-        k, q = i // n_t, i % n_t
-
-        @pl.when(q > 0)
-        def _():
-            x_copy(k, q, peer(q, 1), me_t).wait_send()
-            o_copy(k, q, peer(q, 1), me_t).wait_send()
-        for d, to in lanes:
-            x_ring(q, k, d, to).wait_send()
-            x_next(q, k, d, to).wait_send()
-    for k in range(n_k):
-        for d, to in lanes:
+        for d, to in lanes:
+            x_ring(i % n_t, i // n_t, d, to).wait_send()
+
+    @pl.loop(0, n_t)
+    def _(q):
+        for d, to in lanes:
+            x_next(q, 0, d, to).wait_send()
+    for d, to in lanes:
+        for k in range(n_k):
             o_ring(k, d, to).wait_send()
-            o_next(k, d, to).wait_send()
+        o_next(0, d, to).wait_send()
 
 
 def drain(n, src_ref, out_ref, sems):
@@ -400,6 +434,7 @@
         rows = x_init.shape[0] * x_init.shape[1]
         hid = n_m * hid_dev
         n_k, n_x = rows // (n_t * n_m * ROWS), n_t // 2
+        n_g = n_k + 1
         vmem = pl.BlockSpec(memory_space=pltpu.VMEM)
         sem = lambda *shape: pltpu.SemaphoreType.DMA(shape)
         hbm = pl.BlockSpec(memory_space=pltpu.HBM)
@@ -419,17 +454,17 @@
                 pltpu.VMEM((n_t, span, 128), F32),
                 pltpu.VMEM((n_t, span, hid), F32),
                 pltpu.VMEM((n_t, span, hid), F32),
-                pltpu.VMEM((n_k, n_x, 2 * span * ROWS, chan), BF16),
-                pltpu.VMEM((n_k, n_t, ROWS, chan), F32),
+                pltpu.VMEM((n_g + 1, n_x, 2 * span * ROWS, chan), BF16),
+                pltpu.VMEM((n_g, n_t, ROWS, chan), F32),
                 pltpu.VMEM((n_m, n_k, n_x, 2 * span * ROWS, chan), BF16),
                 pltpu.VMEM((n_m, n_k, n_t, ROWS, chan), F32),
-                pltpu.VMEM((2 * span * ROWS, hid), BF16),
+                pltpu.VMEM((2, 2 * span * ROWS, hid), BF16),
                 sem(6),
                 sem(2, 2), sem(2, 2), sem(2), sem(2), sem(2, 3), sem(2, 3),
                 sem(2, 3), sem(2, 3), sem(n_x), sem(n_x), sem(n_x), sem(n_x), sem(n_t), sem(n_t),
-                sem(n_k, n_t), sem(n_k, n_t),
-                sem(2, n_k * n_t), sem(2, n_k * n_t), sem(2, n_k * n_t), sem(2, n_k * n_t),
-                sem(n_k, n_t), sem(n_k, n_t),
+                sem(n_g, n_t), sem(n_g, n_t),
+                sem(2, n_k * n_t), sem(2, n_k * n_t), sem(2, n_t), sem(2, n_t),
+                sem(n_g, n_t), sem(n_g, n_t),
                 sem(2, n_k), sem(2, n_k), sem(2, n_k), sem(2, n_k),
             ],
             compiler_params=pltpu.CompilerParams(collective_id=0, has_side_effects=True, vmem_limit_bytes=VMEM_BYTES - 4 * span * rows * chan),

time: 128 us -> 127 us (level)
  no operation moved by 1% of the time
where the time goes in v4:
time: 127 us; the launch traced here: 126 us
  Pallas kernels  126 us (99%)
    pallas_call x1, Pallas kernels, device_body(): pl.pallas_call(functools.partial(kernel, n_t, n_m), out_shape=pltpu.VMEM(...  121 us
    pallas_call x1, Pallas kernels, device_body(): pl.pallas_call(functools.partial(drain, STAGES), out_shape=jax.ShapeDtype...  5.95 us

profile of v4, /device:TPU:96, one launch (start us, length us, event | category | flops | bytes accessed | tf_op | source)
XLA Modules:
  0.0 126.5 jit_solution(7377713194859486181)
XLA Ops:
  0.0 120.5 %shard_map.64.src_ref = f32[16,1024,256]{2,1,0:T(8,128)S(1)} custom-call(f32[16]{0:T(128)} %h_hbm.1, f32[1024,256]{1,0:T(8,128)} %bitcast.3, bf16[288,256]{1,0:T(8,128)(2,1)} %bitcast.4, bf16[288,256]{1,0:T(8,128)(2,1)} %wd_hbm.1, bf16[16,288]{1,0:T(8,128)(2,1)} %ms_hbm.1, bf16[16,288]{1,0:T(8,128)(2,1)} %mb_hbm.1), custom_call_target="tpu_custom_call" | custom-call | tf_op jit(solution)/shard_map/pallas_call | solution.py:441
  120.5 6.0 %shard_map.65 = f32[16,1024,256]{2,1,0:T(8,128)} custom-call(f32[16,1024,256]{2,1,0:T(8,128)S(1)} %shard_map.64.src_ref), custom_call_target="tpu_custom_call" | custom-call | tf_op jit(solution)/shard_map/pallas_call | solution.py:472
